TPU v7x, 32 devices: a whole 2x2x4 slice. The times are simulated.
32 devices in a mesh: grp: 4 (over y, x), row: 8 (over z, core).
Axes of the slice: x: 2, y: 2, z: 4, core: 2. Of those that a mesh axis runs over, the one named last changes fastest.
Arguments:
- tiles: bfloat16 [4, 8, 32, 256, 256], P('grp', 'row'), may hold values from -0.046875 to 0.046875
- tile_rows: int32 [4, 8, 32], P('grp', 'row'), may hold values from 0 to 3, as said below
- tile_cols: int32 [4, 8, 32], P('grp', 'row'), may hold values from 0 to 7, as said below
- live_tiles: int32 [4, 8], P('grp', 'row'), may hold values from 16 to 32, as said below
- dual_shift: float32 [8192], P('row'), may hold values from 0.5 to 2
- start_block: float32 [32, 8192], P(None, 'row'), may hold values from -6 to 6
Outputs:
- projections: float32 [4, 32, 128], replicated
- factors: float32 [4, 32, 32], replicated
- next_block: float32 [32, 8192], P(None, 'row')
Inputs may be any that keep to these rules, and one draw needn't show every extreme that they name: `tile_rows`: the tile slots of one device sit at distinct positions (block row, column block), padding slots included. `tile_cols`: column block j of group g is global block column (j // 1) * 4 + g * 1 + j % 1. Slots from live_tiles on are padding with arbitrary values; in every draw some device has all 32 slots live.
All inputs are finite; a program needn't handle non-finite values.
Results may differ from a plain program's by a relative error of at most 0.013.
Values may be sent and summed in bfloat16 or wider, within the bound.
A program may use at most 64 MiB of HBM per device.

v0:
```python
import jax
import jax.numpy as jnp
from jax import lax
from jax.sharding import PartitionSpec as P

ITERS = 4


def inner_product(left, right):
    return lax.dot_general(
        left,
        right,
        (((1,), (1,)), ((), ())),
        precision=lax.Precision.HIGHEST,
        preferred_element_type=jnp.float32,
    )


def apply_matrix(left, right):
    return jnp.dot(left, right, precision=lax.Precision.HIGHEST, preferred_element_type=jnp.float32)


def per_device(tiles, tile_rows, tile_cols, live_tiles, dual_shift, start_block):
    matrix = tiles[0, 0]
    rows_here = tile_rows[0, 0]
    cols_here = tile_cols[0, 0]
    tile_count = matrix.shape[0]
    tile_edge = matrix.shape[1]
    vec_width = start_block.shape[0]
    row_count = start_block.shape[1]
    group_count = lax.axis_size("grp")
    owner_count = lax.axis_size("row")
    owned_blocks = row_count // tile_edge
    quarter_tiles = owned_blocks // group_count
    column_tiles = quarter_tiles * owner_count
    group_index = lax.axis_index("grp")
    live_mask = (jnp.arange(tile_count) < live_tiles[0, 0]).astype(jnp.float32)
    row_table = (rows_here[:, None] == jnp.arange(owned_blocks)[None, :]).astype(
        jnp.float32
    ) * live_mask[:, None]
    col_table = (cols_here[:, None] == jnp.arange(column_tiles)[None, :]).astype(
        jnp.float32
    ) * live_mask[:, None]

    def partial_of(full_rows, group_rows):
        gathered = lax.all_gather(group_rows, "row", axis=1, tiled=True)
        forward = jnp.einsum(
            "kbc,brc->kbr",
            jnp.take(gathered, cols_here, axis=1),
            matrix,
            preferred_element_type=jnp.float32,
        )
        direct = jnp.einsum("kbr,bi->kir", forward, row_table)
        backward = jnp.einsum(
            "kbr,brc->kbc",
            jnp.take(full_rows, rows_here, axis=1),
            matrix,
            preferred_element_type=jnp.float32,
        )
        spread = jnp.einsum("kbc,bj->kjc", backward, col_table)
        mine = lax.psum_scatter(spread, "row", scatter_dimension=1, tiled=True)
        placed = lax.dynamic_update_slice_in_dim(
            jnp.zeros_like(direct), mine, group_index * quarter_tiles, 1
        )
        return 0.5 * (direct + placed)

    def split_parts(vectors):
        rounded = vectors.astype(jnp.bfloat16).reshape(vec_width, owned_blocks, tile_edge)
        return (
            rounded,
            lax.dynamic_slice_in_dim(rounded, group_index * quarter_tiles, quarter_tiles, 1),
        )

    def finish_sum(partial_value):
        return lax.psum(partial_value, "grp").reshape(vec_width, row_count)

    def reduce_dots(values):
        return lax.psum(values, "row")

    def orthonormal(block, gram_matrix):
        lower_factor = jnp.linalg.cholesky(gram_matrix)
        return (
            lax.linalg.triangular_solve(lower_factor, block, left_side=True, lower=True),
            lower_factor,
        )

    current, unused = orthonormal(start_block, reduce_dots(inner_product(start_block, start_block)))
    total_cols = ITERS * vec_width
    basis_rows = jnp.zeros((total_cols, current.shape[1]), jnp.float32)
    projections = jnp.zeros((ITERS, vec_width, total_cols), jnp.float32)
    factors = jnp.zeros((ITERS, vec_width, vec_width), jnp.float32)

    def lanczos_step(step_index, state_now):
        current, basis_rows, projections, factors = state_now
        basis_rows = lax.dynamic_update_slice_in_dim(basis_rows, current, step_index * vec_width, 0)
        full_rows, group_rows = split_parts(current)
        image = finish_sum(partial_of(full_rows, group_rows)) - current * dual_shift[None, :]
        first_coef, square_sum = reduce_dots(
            (inner_product(image, basis_rows), inner_product(image, image))
        )
        image = image - apply_matrix(first_coef, basis_rows)
        gram_matrix = square_sum - inner_product(first_coef, first_coef)
        current, lower_factor = orthonormal(image, gram_matrix)
        projections = lax.dynamic_update_index_in_dim(projections, first_coef, step_index, 0)
        factors = lax.dynamic_update_index_in_dim(factors, lower_factor, step_index, 0)
        return (current, basis_rows, projections, factors)

    current, basis_rows, projections, factors = lax.fori_loop(
        0, ITERS, lanczos_step, (current, basis_rows, projections, factors)
    )
    return (projections, factors, current)


def solution(mesh):
    in_specs = (
        P("grp", "row", None, None, None),
        P("grp", "row", None),
        P("grp", "row", None),
        P("grp", "row"),
        P("row"),
        P(None, "row"),
    )
    out_specs = (P(), P(), P(None, "row"))
    return jax.shard_map(
        per_device, mesh=mesh, in_specs=in_specs, out_specs=out_specs, check_vma=False
    )
```

profile of v0, /device:TPU:0, one launch (start us, length us, event | category | flops | bytes accessed | tf_op | source)
XLA Modules:
  0.0 526.2 jit_solution(8943379851777965999)
XLA Ops:
  7.2 0.9 copy-done
  8.3 30.3 %psum.46 = f32[32,32]{0,1:T(8,128)S(1)} all-reduce(f32[32,32]{0,1:T(8,128)S(1)} %fusion.41), channel_id=1, replica_groups=mesh['grp'=4,'row'=8] {'row'}, use_global_device_ids=true, to_apply=%region_0.0 | all-reduce | flops 1024 | bytes 8192 | tf_op jit(solution)/shard_map/psum | solution.py:78
  38.7 2.9 cholesky.55
  43.0 2.4 custom-call.7
  46.5 472.2 %while.23 = (s32[]{:T(128)}, f32[32,1024]{1,0:T(8,128)S(1)}, f32[128,1024]{1,0:T(8,128)S(1)}, f32[4,32,128]{2,1,0:T(8,128)}, f32[4,32,32]{2,1,0:T(8,128)}, /*ind...) while((s32[]{:T(128)}, f32[32,1024]{1,0:T(8,128)S(1)}, ...), condition=%wide.region_8.11_spmd.clone.clone, body=%wide.region_3.10_spmd.clone.clone.sunk | while | flops 402879840 | bytes 20164480 | solution.py:108
  46.5 0.7 fusion.101
  47.2 0.7 compare_and_fusion.5
  48.5 3.0 convolution_bitcast_fusion.7
  52.0 0.8 copy.64
  52.9 14.0 %all_gather.12 = bf16[32,8,256]{2,0,1:T(8,128)(2,1)S(1)} all-gather(bf16[32,1,256]{2,0,1:T(8,128)(2,1)S(1)} %copy.62), channel_id=1, replica_groups=mesh['grp'=4,'row'=8] {'row'}, dimensions={1}, use_global_device_ids=true | all-gather | bytes 147456 | tf_op jit(solution)/shard_map/while/body/eval_jaxpr/all_gather | solution.py:46
  67.5 3.5 convolution_bitcast_fusion.6
  71.5 10.4 %reduce-scatter.2.cloned.1.call-done = f32[32,1,256]{2,0,1:T(8,128)} async-done(((f32[32,8,256]{2,0,1:T(8,128)}), f32[32,1,256]{2,0,1:T(8,128)}) %reduce-scatter.2.cloned.1.call-update) | async-done | bytes 32784 | tf_op jit(solution)/shard_map/while/body/eval_jaxpr/reduce_scatter | solution.py:61
  81.9 0.8 bitcast_add_fusion.4
  82.9 0.7 copy.65
  83.6 42.2 %all-reduce.5.cloned.1.call-done = f32[32,1024]{1,0:T(8,128)} async-done(((f32[32,1024]{1,0:T(8,128)}), f32[32,1024]{1,0:T(8,128)}) %all-reduce.5.cloned.1.call-update) | async-done | bytes 131088 | tf_op jit(solution)/shard_map/while/body/eval_jaxpr/psum | solution.py:75
  125.9 0.9 constant_dynamic-update-slice_fusion.2
  127.7 28.1 %all-reduce.2 = (f32[32,128]{1,0:T(8,128)S(1)}, f32[32,32]{0,1:T(8,128)S(1)}) all-reduce(f32[32,128]{1,0:T(8,128)S(1)} %fusion.102, f32[32,32]{0,1:T(8,128)S(1)} %fusion.103), channel_id=1, replica_groups=mesh['grp'=4,'row'=8] {'row'}, use_global_device_ids=true, to_apply=%region_7.9 | all-reduce | flops 5120 | bytes 40960 | tf_op jit(solution)/shard_map/while/body/eval_jaxpr/psum | solution.py:78
  156.4 2.9 cholesky.132
  160.7 1.3 bitcast_dynamic-update-slice_fusion.5
  162.0 2.4 custom-call.19
  165.4 0.7 fusion.101
  166.1 0.7 compare_and_fusion.5
  167.4 3.0 convolution_bitcast_fusion.7
  170.8 0.8 copy.64
  171.8 14.0 %all_gather.12 = bf16[32,8,256]{2,0,1:T(8,128)(2,1)S(1)} all-gather(bf16[32,1,256]{2,0,1:T(8,128)(2,1)S(1)} %copy.62), channel_id=1, replica_groups=mesh['grp'=4,'row'=8] {'row'}, dimensions={1}, use_global_device_ids=true | all-gather | bytes 147456 | tf_op jit(solution)/shard_map/while/body/eval_jaxpr/all_gather | solution.py:46
  186.4 3.5 convolution_bitcast_fusion.6
  190.4 9.6 %reduce-scatter.2.cloned.1.call-done = f32[32,1,256]{2,0,1:T(8,128)} async-done(((f32[32,8,256]{2,0,1:T(8,128)}), f32[32,1,256]{2,0,1:T(8,128)}) %reduce-scatter.2.cloned.1.call-update) | async-done | bytes 32784 | tf_op jit(solution)/shard_map/while/body/eval_jaxpr/reduce_scatter | solution.py:61
  200.0 0.8 bitcast_add_fusion.4
  201.0 0.7 copy.65
  201.7 41.9 %all-reduce.5.cloned.1.call-done = f32[32,1024]{1,0:T(8,128)} async-done(((f32[32,1024]{1,0:T(8,128)}), f32[32,1024]{1,0:T(8,128)}) %all-reduce.5.cloned.1.call-update) | async-done | bytes 131088 | tf_op jit(solution)/shard_map/while/body/eval_jaxpr/psum | solution.py:75
  243.6 0.9 constant_dynamic-update-slice_fusion.2
  245.4 28.1 %all-reduce.2 = (f32[32,128]{1,0:T(8,128)S(1)}, f32[32,32]{0,1:T(8,128)S(1)}) all-reduce(f32[32,128]{1,0:T(8,128)S(1)} %fusion.102, f32[32,32]{0,1:T(8,128)S(1)} %fusion.103), channel_id=1, replica_groups=mesh['grp'=4,'row'=8] {'row'}, use_global_device_ids=true, to_apply=%region_7.9 | all-reduce | flops 5120 | bytes 40960 | tf_op jit(solution)/shard_map/while/body/eval_jaxpr/psum | solution.py:78
  274.2 2.9 cholesky.132
  278.4 1.3 bitcast_dynamic-update-slice_fusion.5
  279.7 2.4 custom-call.19
  283.1 0.7 fusion.101
  283.8 0.7 compare_and_fusion.5
  285.1 3.0 convolution_bitcast_fusion.7
  288.5 0.8 copy.64
  289.5 14.0 %all_gather.12 = bf16[32,8,256]{2,0,1:T(8,128)(2,1)S(1)} all-gather(bf16[32,1,256]{2,0,1:T(8,128)(2,1)S(1)} %copy.62), channel_id=1, replica_groups=mesh['grp'=4,'row'=8] {'row'}, dimensions={1}, use_global_device_ids=true | all-gather | bytes 147456 | tf_op jit(solution)/shard_map/while/body/eval_jaxpr/all_gather | solution.py:46
  304.1 3.5 convolution_bitcast_fusion.6
  308.1 9.6 %reduce-scatter.2.cloned.1.call-done = f32[32,1,256]{2,0,1:T(8,128)} async-done(((f32[32,8,256]{2,0,1:T(8,128)}), f32[32,1,256]{2,0,1:T(8,128)}) %reduce-scatter.2.cloned.1.call-update) | async-done | bytes 32784 | tf_op jit(solution)/shard_map/while/body/eval_jaxpr/reduce_scatter | solution.py:61
  317.7 0.8 bitcast_add_fusion.4
  318.7 0.7 copy.65
  319.5 41.9 %all-reduce.5.cloned.1.call-done = f32[32,1024]{1,0:T(8,128)} async-done(((f32[32,1024]{1,0:T(8,128)}), f32[32,1024]{1,0:T(8,128)}) %all-reduce.5.cloned.1.call-update) | async-done | bytes 131088 | tf_op jit(solution)/shard_map/while/body/eval_jaxpr/psum | solution.py:75
  361.3 0.9 constant_dynamic-update-slice_fusion.2
  363.1 28.1 %all-reduce.2 = (f32[32,128]{1,0:T(8,128)S(1)}, f32[32,32]{0,1:T(8,128)S(1)}) all-reduce(f32[32,128]{1,0:T(8,128)S(1)} %fusion.102, f32[32,32]{0,1:T(8,128)S(1)} %fusion.103), channel_id=1, replica_groups=mesh['grp'=4,'row'=8] {'row'}, use_global_device_ids=true, to_apply=%region_7.9 | all-reduce | flops 5120 | bytes 40960 | tf_op jit(solution)/shard_map/while/body/eval_jaxpr/psum | solution.py:78
  391.9 2.9 cholesky.132
  396.1 1.3 bitcast_dynamic-update-slice_fusion.5
  397.4 2.4 custom-call.19
  401.5 0.7 compare_and_fusion.5
  402.8 3.0 convolution_bitcast_fusion.7
  406.3 0.8 copy.64
  407.3 14.0 %all_gather.12 = bf16[32,8,256]{2,0,1:T(8,128)(2,1)S(1)} all-gather(bf16[32,1,256]{2,0,1:T(8,128)(2,1)S(1)} %copy.62), channel_id=1, replica_groups=mesh['grp'=4,'row'=8] {'row'}, dimensions={1}, use_global_device_ids=true | all-gather | bytes 147456 | tf_op jit(solution)/shard_map/while/body/eval_jaxpr/all_gather | solution.py:46
  421.8 3.5 convolution_bitcast_fusion.6
  425.8 9.7 %reduce-scatter.2.cloned.1.call-done = f32[32,1,256]{2,0,1:T(8,128)} async-done(((f32[32,8,256]{2,0,1:T(8,128)}), f32[32,1,256]{2,0,1:T(8,128)}) %reduce-scatter.2.cloned.1.call-update) | async-done | bytes 32784 | tf_op jit(solution)/shard_map/while/body/eval_jaxpr/reduce_scatter | solution.py:61
  435.5 0.8 bitcast_add_fusion.4
  436.5 0.7 copy.65
  437.2 42.0 %all-reduce.5.cloned.1.call-done = f32[32,1024]{1,0:T(8,128)} async-done(((f32[32,1024]{1,0:T(8,128)}), f32[32,1024]{1,0:T(8,128)}) %all-reduce.5.cloned.1.call-update) | async-done | bytes 131088 | tf_op jit(solution)/shard_map/while/body/eval_jaxpr/psum | solution.py:75
  479.2 0.9 constant_dynamic-update-slice_fusion.2
  481.0 28.1 %all-reduce.2 = (f32[32,128]{1,0:T(8,128)S(1)}, f32[32,32]{0,1:T(8,128)S(1)}) all-reduce(f32[32,128]{1,0:T(8,128)S(1)} %fusion.102, f32[32,32]{0,1:T(8,128)S(1)} %fusion.103), channel_id=1, replica_groups=mesh['grp'=4,'row'=8] {'row'}, use_global_device_ids=true, to_apply=%region_7.9 | all-reduce | flops 5120 | bytes 40960 | tf_op jit(solution)/shard_map/while/body/eval_jaxpr/psum | solution.py:78
  509.7 2.9 cholesky.132
  514.0 1.3 bitcast_dynamic-update-slice_fusion.5
  515.3 2.4 custom-call.19
  (159 shorter events, 28.0 us)
Async XLA Ops:
  7.2 0.9 copy-start
  46.5 5.1 copy-start.3
  46.5 35.4 %reduce-scatter.2.cloned.1.call-start = ((), (), s32[]{:S(2)}) async-start(), calls=%async_computation.1 | async-start | bytes 294912 | tf_op jit(solution)/shard_map/while/body/eval_jaxpr/reduce_scatter | solution.py:61
  51.5 19.5 %copy-start.4 = (s32[32]{0:T(128)S(1)}, s32[32]{0:T(128)}, u32[]{:S(2)}) copy-start(s32[32]{0:T(128)} %get-tuple-element.492) | copy-start | bytes 388 | tf_op jit(solution)/shard_map/while
  52.7 73.2 %copy-start.2 = (f32[1024]{0:T(1024)S(1)}, f32[1024]{0:T(1024)}, u32[]{:S(2)}) copy-start(f32[1024]{0:T(1024)} %get-tuple-element.493) | copy-start | bytes 12292 | tf_op jit(solution)/shard_map/while
  52.8 73.1 %all-reduce.5.cloned.1.call-start = ((), (), s32[]{:S(2)}) async-start(), calls=%async_computation.2 | async-start | bytes 262144 | tf_op jit(solution)/shard_map/while/body/eval_jaxpr/psum | solution.py:75
  165.4 5.1 copy-start.3
  165.4 34.6 %reduce-scatter.2.cloned.1.call-start = ((), (), s32[]{:S(2)}) async-start(), calls=%async_computation.1 | async-start | bytes 294912 | tf_op jit(solution)/shard_map/while/body/eval_jaxpr/reduce_scatter | solution.py:61
  170.4 19.5 %copy-start.4 = (s32[32]{0:T(128)S(1)}, s32[32]{0:T(128)}, u32[]{:S(2)}) copy-start(s32[32]{0:T(128)} %get-tuple-element.492) | copy-start | bytes 388 | tf_op jit(solution)/shard_map/while
  171.6 72.0 %copy-start.2 = (f32[1024]{0:T(1024)S(1)}, f32[1024]{0:T(1024)}, u32[]{:S(2)}) copy-start(f32[1024]{0:T(1024)} %get-tuple-element.493) | copy-start | bytes 12292 | tf_op jit(solution)/shard_map/while
  171.6 72.0 %all-reduce.5.cloned.1.call-start = ((), (), s32[]{:S(2)}) async-start(), calls=%async_computation.2 | async-start | bytes 262144 | tf_op jit(solution)/shard_map/while/body/eval_jaxpr/psum | solution.py:75
  283.1 5.1 copy-start.3
  283.1 34.6 %reduce-scatter.2.cloned.1.call-start = ((), (), s32[]{:S(2)}) async-start(), calls=%async_computation.1 | async-start | bytes 294912 | tf_op jit(solution)/shard_map/while/body/eval_jaxpr/reduce_scatter | solution.py:61
  288.1 19.5 %copy-start.4 = (s32[32]{0:T(128)S(1)}, s32[32]{0:T(128)}, u32[]{:S(2)}) copy-start(s32[32]{0:T(128)} %get-tuple-element.492) | copy-start | bytes 388 | tf_op jit(solution)/shard_map/while
  289.3 72.0 %copy-start.2 = (f32[1024]{0:T(1024)S(1)}, f32[1024]{0:T(1024)}, u32[]{:S(2)}) copy-start(f32[1024]{0:T(1024)} %get-tuple-element.493) | copy-start | bytes 12292 | tf_op jit(solution)/shard_map/while
  289.3 72.0 %all-reduce.5.cloned.1.call-start = ((), (), s32[]{:S(2)}) async-start(), calls=%async_computation.2 | async-start | bytes 262144 | tf_op jit(solution)/shard_map/while/body/eval_jaxpr/psum | solution.py:75
  400.8 5.1 copy-start.3
  400.8 34.6 %reduce-scatter.2.cloned.1.call-start = ((), (), s32[]{:S(2)}) async-start(), calls=%async_computation.1 | async-start | bytes 294912 | tf_op jit(solution)/shard_map/while/body/eval_jaxpr/reduce_scatter | solution.py:61
  405.9 19.5 %copy-start.4 = (s32[32]{0:T(128)S(1)}, s32[32]{0:T(128)}, u32[]{:S(2)}) copy-start(s32[32]{0:T(128)} %get-tuple-element.492) | copy-start | bytes 388 | tf_op jit(solution)/shard_map/while
  407.0 72.1 %copy-start.2 = (f32[1024]{0:T(1024)S(1)}, f32[1024]{0:T(1024)}, u32[]{:S(2)}) copy-start(f32[1024]{0:T(1024)} %get-tuple-element.493) | copy-start | bytes 12292 | tf_op jit(solution)/shard_map/while
  407.1 72.1 %all-reduce.5.cloned.1.call-start = ((), (), s32[]{:S(2)}) async-start(), calls=%async_computation.2 | async-start | bytes 262144 | tf_op jit(solution)/shard_map/while/body/eval_jaxpr/psum | solution.py:75
  518.7 0.7 copy-start.1
Sparse Core Ops, SparseCore 0:
  52.9 28.9 reduce-scatter.1
  85.3 40.4 all-reduce.4
  171.7 28.1 reduce-scatter.1
  203.3 40.2 all-reduce.4
  289.5 28.2 reduce-scatter.1
  321.0 40.2 all-reduce.4
  407.2 28.2 reduce-scatter.1
  438.9 40.2 all-reduce.4
where the time goes:
time: 527 us; the launch traced here: 526 us
  waiting for transfers between devices  207 us (39%)
  blocking collectives  199 us (38%)
  other arithmetic  51 us (10%)
  matrix products  36.9 us (7%)
  local copies, waits for them, and re-layouts  16 us (3%)
  between operations  14.7 us (3%)
    psum x4, waiting for transfers between devices, finish_sum(): return lax.psum(partial_value, 'grp').reshape(vec_width, row_count)  168 us
    psum x5, blocking collectives, reduce_dots(): return lax.psum(values, 'row')  143 us
    all_gather x4, blocking collectives, partial_of(): gathered = lax.all_gather(group_rows, 'row', axis=1, tiled=True)  56 us
    reduce_scatter x4, waiting for transfers between devices, partial_of(): mine = lax.psum_scatter(spread, 'row', scatter_dimension=1, tiled=True)  39.4 us
    another operation x15, other arithmetic, orthonormal(): lower_factor = jnp.linalg.cholesky(gram_matrix)  18 us
    another operation x10, other arithmetic, orthonormal(): lax.linalg.triangular_solve(lower_factor, block, left_side=True, lower=True)  15.4 us
    dot_general x4, matrix products, partial_of(): jnp.einsum('kbc,brc->kbr', jnp.take(gathered, cols_here, axis=1), matrix,...  14.2 us
    dot_general x4, matrix products, partial_of(): jnp.einsum('kbr,brc->kbc', jnp.take(full_rows, rows_here, axis=1), matrix...  12.1 us
  transfers between devices with their start and end apart: 8, of which 8 were waited for; matrix products, arithmetic and copies ran while one was open for 4% of the time, Pallas kernels for 0%

commit v1 on v0

v1 whole, which is shorter than its diff:
```python
import functools

import jax
import jax.numpy as jnp
from jax import lax
from jax.experimental import pallas as pl
from jax.experimental.pallas import tpu as pltpu
from jax.sharding import PartitionSpec as P

ITERS = 4
MESH = pl.DeviceIdType.MESH
HIGH = lax.Precision.HIGHEST
NT = (((1,), (1,)), ((), ()))


def dot_nt(a, b):
    return lax.dot_general(a, b, NT, precision=HIGH, preferred_element_type=jnp.float32)


def dot_nn(a, b):
    return jnp.dot(a, b, precision=HIGH, preferred_element_type=jnp.float32)


def factor_and_inverse(gram):
    n = gram.shape[0]
    row = lax.broadcasted_iota(jnp.int32, (n, 2 * n), 0)
    lane = lax.broadcasted_iota(jnp.int32, (n, 2 * n), 1)
    work = jnp.concatenate([gram, jnp.where(row == lane, 1.0, 0.0)[:, :n]], axis=1)
    lower = jnp.zeros((n, n), jnp.float32)
    pivots = jnp.zeros((n, 2 * n), jnp.float32)
    for k in range(n):
        column = jnp.broadcast_to(work[:, k : k + 1], (n, 2 * n))
        pivot_row = work[k : k + 1, :]
        pivot = column[k : k + 1, :]
        scale = 1.0 / pivot
        below = jnp.where(row > k, column, 0.0)
        lower = jnp.where((lane[:, :n] == k) & (row[:, :n] >= k), column[:, :n] * lax.rsqrt(pivot[:, :n]), lower)
        pivots = jnp.where(row == k, pivot, pivots)
        work = work - below * (pivot_row * scale)
    inverse = (work * lax.rsqrt(pivots))[:, n:]
    return lower, inverse


def kernel(
    steps, group_count, owner_count,
    start_ref, shift_ref, place_ref, tiles_ref,
    proj_ref, fac_ref, next_ref,
    dense, gathered, own, back_out, back_in, direct_out, direct_in,
    dots_grp, dots_row, basis, current, last,
    gather_row_send, gather_row_recv, gather_grp_send, gather_grp_recv,
    back_send, back_recv, direct_send, direct_recv,
    dgrp_send, dgrp_recv, drow_send, drow_recv, last_send, last_recv,
):
    g = lax.axis_index("grp")
    r = lax.axis_index("row")
    width = start_ref.shape[0]
    row_count = start_ref.shape[1]
    part = row_count // group_count
    edge = tiles_ref.shape[1]
    owned = row_count // edge
    per_part = part // edge
    row_peers = [lax.rem(r + d, owner_count) for d in range(1, owner_count)]
    grp_peers = [lax.rem(g + d, group_count) for d in range(1, group_count)]

    barrier = pltpu.get_barrier_semaphore()
    for peer in row_peers:
        pl.semaphore_signal(barrier, inc=1, device_id=(g, peer), device_id_type=MESH)
    for peer in grp_peers:
        pl.semaphore_signal(barrier, inc=1, device_id=(peer, r), device_id_type=MESH)
    pl.semaphore_wait(barrier, len(row_peers) + len(grp_peers))

    def to_row(peer, src, dst, send, recv):
        return pltpu.make_async_remote_copy(
            src_ref=src, dst_ref=dst, send_sem=send, recv_sem=recv,
            device_id=(g, peer), device_id_type=MESH,
        )

    def to_grp(peer, src, dst, send, recv):
        return pltpu.make_async_remote_copy(
            src_ref=src, dst_ref=dst, send_sem=send, recv_sem=recv,
            device_id=(peer, r), device_id_type=MESH,
        )

    def sum_over_row(value):
        dots_row[r] = value
        sends = []
        for peer in row_peers:
            copy = to_row(peer, dots_row.at[r], dots_row.at[r], drow_send.at[peer], drow_recv.at[r])
            copy.start()
            sends.append(copy)
        for peer in row_peers:
            to_row(peer, dots_row.at[peer], dots_row.at[peer], drow_send.at[peer], drow_recv.at[peer]).wait_recv()
        total = dots_row[0]
        for index in range(1, owner_count):
            total = total + dots_row[index]
        for copy in sends:
            copy.wait_send()
        return total

    def sum_over_grp(value):
        dots_grp[g] = value
        sends = []
        for peer in grp_peers:
            copy = to_grp(peer, dots_grp.at[g], dots_grp.at[g], dgrp_send.at[peer], dgrp_recv.at[g])
            copy.start()
            sends.append(copy)
        for peer in grp_peers:
            to_grp(peer, dots_grp.at[peer], dots_grp.at[peer], dgrp_send.at[peer], dgrp_recv.at[peer]).wait_recv()
        total = dots_grp[0]
        for index in range(1, group_count):
            total = total + dots_grp[index]
        for copy in sends:
            copy.wait_send()
        return total

    fold = 128 // width

    def pack(square):
        height = width // fold
        return jnp.concatenate([square[i * height : (i + 1) * height] for i in range(fold)], axis=1)

    def unpack(packed):
        return jnp.concatenate([packed[:, i * width : (i + 1) * width] for i in range(fold)], axis=0)

    total_cols = steps * width
    start = start_ref[...]
    start_gram = pack(dot_nt(start, start))
    start_sum = sum_over_row(
        jnp.concatenate([jnp.zeros((width, total_cols), jnp.float32), start_gram], axis=0)
    )
    for j in range(owner_count * per_part):
        for i in range(owned):
            slot = place_ref[i * owner_count * per_part + j]
            keep = jnp.where(slot > 0, 1.0, 0.0).astype(jnp.bfloat16)
            tile = tiles_ref[jnp.maximum(slot - 1, 0)]
            dense[
                j // per_part,
                i * edge : (i + 1) * edge,
                (j % per_part) * edge : (j % per_part + 1) * edge,
            ] = tile * keep
    basis[...] = jnp.zeros_like(basis)
    proj_ref[...] = jnp.zeros_like(proj_ref)
    unused, inverse = factor_and_inverse(unpack(start_sum[width:]))
    mine = pl.ds(pl.multiple_of(g * part, part), part)
    current[...] = dot_nn(inverse, start_ref[:, mine])
    shift = shift_ref[:, mine]

    def step_body(step, carry):
        now = current[...]
        basis[pl.ds(pl.multiple_of(step * width, width), width), :] = now
        rounded = now.astype(jnp.bfloat16)
        own[g] = rounded
        gathered[r] = rounded
        sends = []
        for peer in grp_peers:
            copy = to_grp(peer, own.at[g], own.at[g], gather_grp_send.at[peer], gather_grp_recv.at[g])
            copy.start()
            sends.append(copy)
        for peer in row_peers:
            copy = to_row(peer, gathered.at[r], gathered.at[r], gather_row_send.at[peer], gather_row_recv.at[r])
            copy.start()
            sends.append(copy)
        for peer in grp_peers:
            to_grp(peer, own.at[peer], own.at[peer], gather_grp_send.at[peer], gather_grp_recv.at[peer]).wait_recv()
        full = jnp.concatenate([own[i] for i in range(group_count)], axis=1)
        for peer in row_peers:
            back_out[peer] = jnp.dot(full, dense[peer], preferred_element_type=jnp.float32).astype(jnp.bfloat16)
            copy = to_row(peer, back_out.at[peer], back_in.at[r], back_send.at[peer], back_recv.at[r])
            copy.start()
            sends.append(copy)
        total = jnp.dot(full, dense[r], preferred_element_type=jnp.float32)
        for peer in row_peers:
            to_row(peer, gathered.at[peer], gathered.at[peer], gather_row_send.at[peer], gather_row_recv.at[peer]).wait_recv()

        def forward(quarter):
            rows = pl.ds(pl.multiple_of(quarter * part, part), part)
            value = jnp.zeros((width, part), jnp.float32)
            for j in range(owner_count):
                value = value + lax.dot_general(
                    gathered[j], dense[j, rows, :], NT, preferred_element_type=jnp.float32
                )
            return value

        for peer in grp_peers:
            direct_out[peer] = forward(peer).astype(jnp.bfloat16)
            copy = to_grp(peer, direct_out.at[peer], direct_in.at[g], direct_send.at[peer], direct_recv.at[g])
            copy.start()
            sends.append(copy)
        total = total + forward(g)
        for peer in row_peers:
            to_row(peer, back_out.at[peer], back_in.at[peer], back_send.at[peer], back_recv.at[peer]).wait_recv()
            total = total + back_in[peer].astype(jnp.float32)
        for peer in grp_peers:
            to_grp(peer, direct_out.at[peer], direct_in.at[peer], direct_send.at[peer], direct_recv.at[peer]).wait_recv()
            total = total + direct_in[peer].astype(jnp.float32)
        for copy in sends:
            copy.wait_send()
        image = 0.5 * total - now * shift

        dots = dot_nt(image, jnp.concatenate([basis[...], image], axis=0))
        packed = jnp.concatenate([dots[:, :total_cols], pack(dots[:, total_cols:])], axis=0)
        summed = sum_over_row(sum_over_grp(packed))
        first = summed[:width]
        gram = unpack(summed[width:]) - dot_nt(first, first)
        image = image - dot_nn(first, basis[...])
        lower, inverse = factor_and_inverse(gram)
        current[...] = dot_nn(inverse, image)
        proj_ref[step] = first
        fac_ref[step] = lower
        return carry

    lax.fori_loop(0, steps, step_body, 0)

    last[g] = current[...]
    sends = []
    for peer in grp_peers:
        copy = to_grp(peer, last.at[g], last.at[g], last_send.at[peer], last_recv.at[g])
        copy.start()
        sends.append(copy)
    for peer in grp_peers:
        to_grp(peer, last.at[peer], last.at[peer], last_send.at[peer], last_recv.at[peer]).wait_recv()
    for index in range(group_count):
        next_ref[:, index * part : (index + 1) * part] = last[index]
    for copy in sends:
        copy.wait_send()


def per_device(tiles, tile_rows, tile_cols, live_tiles, dual_shift, start_block):
    matrix = tiles[0, 0]
    tile_count, edge = matrix.shape[0], matrix.shape[1]
    width, row_count = start_block.shape
    group_count = lax.axis_size("grp")
    owner_count = lax.axis_size("row")
    owned = row_count // edge
    part = row_count // group_count
    columns = part // edge * owner_count
    total_cols = ITERS * width
    order = jnp.arange(tile_count, dtype=jnp.int32)
    position = tile_rows[0, 0] * columns + tile_cols[0, 0]
    here = (position[None, :] == jnp.arange(owned * columns, dtype=jnp.int32)[:, None]) & (
        order < live_tiles[0, 0]
    )[None, :]
    place = jnp.sum(jnp.where(here, order[None, :] + 1, 0), axis=1).astype(jnp.int32)

    vmem = pl.BlockSpec(memory_space=pltpu.VMEM)
    smem = pl.BlockSpec(memory_space=pltpu.SMEM)
    dma = pltpu.SemaphoreType.DMA
    packed = width + width * width // 128
    grp_sem = dma((group_count,))
    row_sem = dma((owner_count,))
    return pl.pallas_call(
        functools.partial(kernel, ITERS, group_count, owner_count),
        out_shape=(
            jax.ShapeDtypeStruct((ITERS, width, total_cols), jnp.float32),
            jax.ShapeDtypeStruct((ITERS, width, width), jnp.float32),
            jax.ShapeDtypeStruct((width, row_count), jnp.float32),
        ),
        in_specs=[vmem, vmem, smem, vmem],
        out_specs=(vmem, vmem, vmem),
        scratch_shapes=[
            pltpu.VMEM((owner_count, row_count, part), jnp.bfloat16),
            pltpu.VMEM((owner_count, width, part), jnp.bfloat16),
            pltpu.VMEM((group_count, width, part), jnp.bfloat16),
            pltpu.VMEM((owner_count, width, part), jnp.bfloat16),
            pltpu.VMEM((owner_count, width, part), jnp.bfloat16),
            pltpu.VMEM((group_count, width, part), jnp.bfloat16),
            pltpu.VMEM((group_count, width, part), jnp.bfloat16),
            pltpu.VMEM((group_count, packed, total_cols), jnp.float32),
            pltpu.VMEM((owner_count, packed, total_cols), jnp.float32),
            pltpu.VMEM((total_cols, part), jnp.float32),
            pltpu.VMEM((width, part), jnp.float32),
            pltpu.VMEM((group_count, width, part), jnp.float32),
            row_sem, row_sem, grp_sem, grp_sem,
            row_sem, row_sem, grp_sem, grp_sem,
            grp_sem, grp_sem, row_sem, row_sem, grp_sem, grp_sem,
        ],
        compiler_params=pltpu.CompilerParams(
            collective_id=0, has_side_effects=True, vmem_limit_bytes=60 * 1024 * 1024
        ),
    )(start_block, dual_shift[None, :], place, matrix)


def solution(mesh):
    in_specs = (
        P("grp", "row", None, None, None),
        P("grp", "row", None),
        P("grp", "row", None),
        P("grp", "row"),
        P("row"),
        P(None, "row"),
    )
    out_specs = (P(), P(), P(None, "row"))
    return jax.shard_map(
        per_device, mesh=mesh, in_specs=in_specs, out_specs=out_specs, check_vma=False
    )
```

time: 527 us -> 113 us (0.21)
  waiting for transfers between devices: 207 us -> 0 us
  blocking collectives: 199 us -> 0 us
  Pallas kernels: 0 us -> 106 us
  other arithmetic: 51 us -> 1.32 us
  matrix products: 36.9 us -> 0 us
  between operations: 14.7 us -> 1.29 us
  local copies, waits for them, and re-layouts: 16 us -> 4.51 us
    psum x4 -> x0, waiting for transfers between devices: 168 us -> none  [finish_sum(): return lax.psum(partial_value, 'grp').reshape(vec_width, row_count)]
    psum x5 -> x0, blocking collectives: 143 us -> none  [reduce_dots(): return lax.psum(values, 'row')]
    pallas_call x0 -> x1, Pallas kernels: none -> 106 us  [per_device(): pl.pallas_call(functools.partial(kernel, ITERS, group_count, owner_count)...]
    all_gather x4 -> x0, blocking collectives: 56 us -> none  [partial_of(): gathered = lax.all_gather(group_rows, 'row', axis=1, tiled=True)]
    reduce_scatter x4 -> x0, waiting for transfers between devices: 39.4 us -> none  [partial_of(): mine = lax.psum_scatter(spread, 'row', scatter_dimension=1, tiled=True)]
    dot_general x33 -> x0, matrix products: 35.4 us -> none  [the longest x4 14.2 us: partial_of(): jnp.einsum('kbc,brc->kbr', jnp.take(gathered, cols_here, axis=1), matrix,...]
    another operation x25 -> x0, other arithmetic: 33.4 us -> none  [the longest x15 18 us: orthonormal(): lower_factor = jnp.linalg.cholesky(gram_matrix)]
    dynamic_update_slice x12 -> x0, other arithmetic: 12 us -> none  [the longest x4 5.04 us: lanczos_step(): lax.dynamic_update_index_in_dim(factors, lower_factor, step_index, 0)]
  transfers between devices with their start and end apart: 8 -> 0, of which waited for: 8 -> 0; matrix products, arithmetic and copies ran while one was open for 4% -> 0% of each run, Pallas kernels for 0% -> 0%
where the time goes in v1:
time: 113 us
  Pallas kernels  106 us (94%)
  local copies, waits for them, and re-layouts  4.51 us (4%)
  other arithmetic  1.32 us (1%)
  between operations  1.29 us (1%)
    pallas_call x1, Pallas kernels, per_device(): pl.pallas_call(functools.partial(kernel, ITERS, group_count, owner_count)...  106 us
    unnamed x3, local copies, waits for them, and re-layouts  4.51 us

profile of v1, /device:TPU:0, one launch (start us, length us, event | category | flops | bytes accessed | tf_op | source)
XLA Modules:
  0.0 112.7 jit_solution(12123620341158160939)
XLA Ops:
  1.3 0.7 add_bitcast_fusion
  2.0 0.6 select_reduce_fusion.place_ref
  2.6 105.6 %shard_map.85 = (f32[4,32,128]{2,1,0:T(8,128)}, f32[4,32,32]{2,1,0:T(8,128)}, f32[32,1024]{1,0:T(8,128)}) custom-call(f32[32,1024]{1,0:T(8,128)} %start_ref.1, f32[1,1024]{1,0:T(1,128)} %bitcast.7, s32[32]{0:T(128)} %select_reduce_fusion.place_ref, bf16[32,256,256]{2,1,0:T(8,128)(2,1)} %bitcast.6), custom_call_target="tpu_custom_call" | custom-call | tf_op jit(solution)/shard_map/pallas_call | solution.py:251
  108.2 1.5 %copy.13 = f32[4,32,128]{2,1,0:T(8,128)} copy(f32[4,32,128]{2,1,0:T(8,128)} %get-tuple-element.6) | data formatting | bytes 131072
  109.7 1.5 %copy.14 = f32[4,32,32]{2,1,0:T(8,128)} copy(f32[4,32,32]{2,1,0:T(8,128)} %get-tuple-element.7) | data formatting | bytes 32768
  111.2 1.6 %copy.15 = f32[32,1024]{1,0:T(8,128)} copy(f32[32,1024]{1,0:T(8,128)} %get-tuple-element.8) | data formatting | bytes 262144
  (2 shorter events, 0.0 us)

commit v2 on v1

v2 whole, which is shorter than its diff:
```python
import functools

import jax
import jax.numpy as jnp
from jax import lax
from jax.experimental import pallas as pl
from jax.experimental.pallas import tpu as pltpu
from jax.sharding import PartitionSpec as P

ITERS = 4
MESH = pl.DeviceIdType.MESH
HIGH = lax.Precision.HIGHEST
NT = (((1,), (1,)), ((), ()))


def dot_nt(a, b):
    return lax.dot_general(a, b, NT, precision=HIGH, preferred_element_type=jnp.float32)


def dot_nn(a, b):
    return jnp.dot(a, b, precision=HIGH, preferred_element_type=jnp.float32)


def factor_and_inverse(gram):
    n = gram.shape[0]
    row = lax.broadcasted_iota(jnp.int32, (n, 2 * n), 0)
    lane = lax.broadcasted_iota(jnp.int32, (n, 2 * n), 1)
    work = jnp.concatenate([gram, jnp.where(row == lane, 1.0, 0.0)[:, :n]], axis=1)
    lower = jnp.zeros((n, n), jnp.float32)
    pivots = jnp.zeros((n, 2 * n), jnp.float32)
    for k in range(n):
        column = jnp.broadcast_to(work[:, k : k + 1], (n, 2 * n))
        pivot_row = work[k : k + 1, :]
        pivot = column[k : k + 1, :]
        scale = 1.0 / pivot
        below = jnp.where(row > k, column, 0.0)
        lower = jnp.where((lane[:, :n] == k) & (row[:, :n] >= k), column[:, :n] * lax.rsqrt(pivot[:, :n]), lower)
        pivots = jnp.where(row == k, pivot, pivots)
        work = work - below * (pivot_row * scale)
    inverse = (work * lax.rsqrt(pivots))[:, n:]
    return lower, inverse


def kernel(
    steps, group_count, owner_count,
    start_ref, shift_ref, place_ref, tiles_hbm,
    proj_ref, fac_ref, next_ref,
    tiles_ref, dense, gathered, own, back_out, back_in, direct_out, direct_in,
    pair_out, pair_in, dots_pair, dots_grp, dots_row, basis, images, current, last, tile_sem,
    gather_row_send, gather_row_recv, gather_grp_send, gather_grp_recv,
    back_send, back_recv, direct_send, direct_recv,
    dgrp_send, dgrp_recv, drow_send, drow_recv, last_send, last_recv,
    relay_send, pair_send, pair_recv, dpair_send, dpair_recv,
):
    g = lax.axis_index("grp")
    r = lax.axis_index("row")
    width = start_ref.shape[0]
    row_count = start_ref.shape[1]
    part = row_count // group_count
    edge = tiles_ref.shape[1]
    owned = row_count // edge
    per_part = part // edge
    chips = owner_count // 2
    chip, core = r // 2, lax.rem(r, 2)
    partner = chip * 2 + 1 - core
    chip_peers = [lax.rem(chip + d, chips) for d in range(1, chips)]
    row_peers = [peer * 2 + core for peer in chip_peers] + [partner]
    grp_peers = [lax.rem(g + d, group_count) for d in range(1, group_count)]

    load = pltpu.make_async_copy(tiles_hbm, tiles_ref, tile_sem)
    load.start()
    barrier = pltpu.get_barrier_semaphore()
    for peer in row_peers:
        pl.semaphore_signal(barrier, inc=1, device_id=(g, peer), device_id_type=MESH)
    for peer in grp_peers:
        pl.semaphore_signal(barrier, inc=1, device_id=(peer, r), device_id_type=MESH)
    pl.semaphore_wait(barrier, len(row_peers) + len(grp_peers))

    def to_row(peer, src, dst, send, recv):
        return pltpu.make_async_remote_copy(
            src_ref=src, dst_ref=dst, send_sem=send, recv_sem=recv,
            device_id=(g, peer), device_id_type=MESH,
        )

    def to_grp(peer, src, dst, send, recv):
        return pltpu.make_async_remote_copy(
            src_ref=src, dst_ref=dst, send_sem=send, recv_sem=recv,
            device_id=(peer, r), device_id_type=MESH,
        )

    def send_grp_dots(value):
        dots_grp[g] = value
        sends = []
        for peer in grp_peers:
            copy = to_grp(peer, dots_grp.at[g], dots_grp.at[g], dgrp_send.at[peer], dgrp_recv.at[g])
            copy.start()
            sends.append(copy)
        return sends

    def take_grp_dots():
        for peer in grp_peers:
            to_grp(peer, dots_grp.at[peer], dots_grp.at[peer], dgrp_send.at[peer], dgrp_recv.at[peer]).wait_recv()
        total = dots_grp[0]
        for index in range(1, group_count):
            total = total + dots_grp[index]
        return total

    def send_pair_dots(half, value):
        dots_pair[half, core] = value
        copy = to_row(
            partner, dots_pair.at[half, core], dots_pair.at[half, core], dpair_send, dpair_recv.at[half]
        )
        copy.start()
        return [copy]

    def send_row_dots(half):
        to_row(
            partner, dots_pair.at[half, 1 - core], dots_pair.at[half, 1 - core], dpair_send, dpair_recv.at[half]
        ).wait_recv()
        dots_row[half, chip] = dots_pair[half, 0] + dots_pair[half, 1]
        sends = []
        for peer in chip_peers:
            copy = to_row(
                peer * 2 + core, dots_row.at[half, chip], dots_row.at[half, chip],
                drow_send.at[peer], drow_recv.at[half, chip],
            )
            copy.start()
            sends.append(copy)
        return sends

    def take_row_dots(half):
        for peer in chip_peers:
            to_row(
                peer * 2 + core, dots_row.at[half, peer], dots_row.at[half, peer],
                drow_send.at[peer], drow_recv.at[half, peer],
            ).wait_recv()
        total = dots_row[half, 0]
        for index in range(1, chips):
            total = total + dots_row[half, index]
        return total

    fold = 128 // width

    def pack(square):
        height = width // fold
        return jnp.concatenate([square[i * height : (i + 1) * height] for i in range(fold)], axis=1)

    def unpack(packed):
        return jnp.concatenate([packed[:, i * width : (i + 1) * width] for i in range(fold)], axis=0)

    total_cols = steps * width

    def local_dots(block):
        dots = dot_nt(block, jnp.concatenate([basis[...], block], axis=0))
        return jnp.concatenate([dots[:, :total_cols], pack(dots[:, total_cols:])], axis=0)

    def finish_dots(summed):
        first = summed[:width]
        gram = unpack(summed[width:]) - dot_nt(first, first)
        lower, inverse = factor_and_inverse(gram)
        return first, lower, inverse

    basis[...] = jnp.zeros_like(basis)
    images[...] = jnp.zeros_like(images)
    mine = pl.ds(pl.multiple_of(g * part, part), part)
    current[...] = start_ref[:, mine]
    load.wait()
    for j in range(owner_count * per_part):
        for i in range(owned):
            slot = place_ref[i * owner_count * per_part + j]
            keep = jnp.where(slot > 0, 1.0, 0.0).astype(jnp.bfloat16)
            tile = tiles_ref[jnp.maximum(slot - 1, 0)]
            dense[
                j // per_part,
                i * edge : (i + 1) * edge,
                (j % per_part) * edge : (j % per_part + 1) * edge,
            ] = tile * keep

    def both(value):
        return value[:width] + value[width:]

    def step_body(step, carry):
        half = lax.rem(step, 2)
        block = current[...]
        high = block.astype(jnp.bfloat16)
        rest = (block - high.astype(jnp.float32)).astype(jnp.bfloat16)
        split = jnp.concatenate([high, rest], axis=0)
        own[g] = split
        gathered[half, r] = split
        sends = []
        for peer in grp_peers:
            copy = to_grp(peer, own.at[g], own.at[g], gather_grp_send.at[peer], gather_grp_recv.at[g])
            copy.start()
            sends.append(copy)
        for peer in row_peers:
            copy = to_row(
                peer, gathered.at[half, r], gathered.at[half, r],
                gather_row_send.at[peer], gather_row_recv.at[half, r],
            )
            copy.start()
            sends.append(copy)
        sends += send_grp_dots(local_dots(block))
        for peer in grp_peers:
            to_grp(peer, own.at[peer], own.at[peer], gather_grp_send.at[peer], gather_grp_recv.at[peer]).wait_recv()
        full = jnp.concatenate([own[i] for i in range(group_count)], axis=1)
        for peer in chip_peers + [chip]:
            pair_out[peer] = both(
                jnp.dot(full, dense[peer * 2 + 1 - core], preferred_element_type=jnp.float32)
            )
            copy = to_row(
                partner, pair_out.at[peer], pair_in.at[half, peer], pair_send.at[peer], pair_recv.at[half, peer]
            )
            copy.start()
            sends.append(copy)
        kept = [
            both(jnp.dot(full, dense[peer * 2 + core], preferred_element_type=jnp.float32))
            for peer in chip_peers
        ]

        def take_pair(peer):
            to_row(
                partner, pair_out.at[peer], pair_in.at[half, peer], pair_send.at[peer], pair_recv.at[half, peer]
            ).wait_recv()
            return pair_in[half, peer]

        for peer, value in zip(chip_peers, kept):
            back_out[peer] = value + take_pair(peer)
            copy = to_row(
                peer * 2 + core, back_out.at[peer], back_in.at[half, chip],
                back_send.at[peer], back_recv.at[half, chip],
            )
            copy.start()
            sends.append(copy)
        sends += send_pair_dots(half, take_grp_dots())
        for peer in chip_peers:
            slot = peer * 2 + core
            to_row(
                slot, gathered.at[half, slot], gathered.at[half, slot],
                gather_row_send.at[slot], gather_row_recv.at[half, slot],
            ).wait_recv()
            copy = to_row(
                partner, gathered.at[half, slot], gathered.at[half, slot],
                relay_send.at[peer], gather_row_recv.at[half, slot],
            )
            copy.start()
            sends.append(copy)
        sends += send_row_dots(half)
        total = both(jnp.dot(full, dense[r], preferred_element_type=jnp.float32)) + take_pair(chip)
        for peer in chip_peers + [chip]:
            slot = peer * 2 + 1 - core
            to_row(
                partner, gathered.at[half, slot], gathered.at[half, slot],
                relay_send.at[peer], gather_row_recv.at[half, slot],
            ).wait_recv()

        def forward(quarter):
            rows = pl.ds(pl.multiple_of(quarter * part, part), part)
            value = jnp.zeros((2 * width, part), jnp.float32)
            for j in range(owner_count):
                value = value + lax.dot_general(
                    gathered[half, j], dense[j, rows, :], NT, preferred_element_type=jnp.float32
                )
            return both(value)

        for peer in grp_peers:
            direct_out[peer] = forward(peer)
            copy = to_grp(peer, direct_out.at[peer], direct_in.at[g], direct_send.at[peer], direct_recv.at[g])
            copy.start()
            sends.append(copy)
        total = total + forward(g)

        first, lower, inverse = finish_dots(take_row_dots(half))
        last_step = jnp.maximum(step - 1, 0)
        proj_ref[last_step] = first
        fac_ref[last_step] = lower
        now = dot_nn(inverse, block - dot_nn(first, basis[...]))

        for peer in chip_peers:
            to_row(
                peer * 2 + core, back_out.at[peer], back_in.at[half, peer],
                back_send.at[peer], back_recv.at[half, peer],
            ).wait_recv()
            total = total + back_in[half, peer]
        for peer in grp_peers:
            to_grp(peer, direct_out.at[peer], direct_in.at[peer], direct_send.at[peer], direct_recv.at[peer]).wait_recv()
            total = total + direct_in[peer]
        image = dot_nn(inverse, 0.5 * total - dot_nn(first, images[...]))
        place = pl.ds(pl.multiple_of(step * width, width), width)
        basis[place, :] = now
        images[place, :] = image
        current[...] = image - now * shift_ref[:, mine]
        for copy in sends:
            copy.wait_send()
        return carry

    lax.fori_loop(0, steps, step_body, 0)

    block = current[...]
    sends = send_grp_dots(local_dots(block))
    sends += send_pair_dots(steps % 2, take_grp_dots())
    sends += send_row_dots(steps % 2)
    block_parts = take_row_dots(steps % 2)
    first, lower, inverse = finish_dots(block_parts)
    proj_ref[steps - 1] = first
    fac_ref[steps - 1] = lower
    last[g] = dot_nn(inverse, block - dot_nn(first, basis[...]))
    for peer in grp_peers:
        copy = to_grp(peer, last.at[g], last.at[g], last_send.at[peer], last_recv.at[g])
        copy.start()
        sends.append(copy)
    for peer in grp_peers:
        to_grp(peer, last.at[peer], last.at[peer], last_send.at[peer], last_recv.at[peer]).wait_recv()
    for index in range(group_count):
        next_ref[:, index * part : (index + 1) * part] = last[index]
    for copy in sends:
        copy.wait_send()


def hand_on(proj_in, fac_in, next_in, proj_ref, fac_ref, next_ref):
    proj_ref[...] = proj_in[...]
    fac_ref[...] = fac_in[...]
    next_ref[...] = next_in[...]


def per_device(tiles, tile_rows, tile_cols, live_tiles, dual_shift, start_block):
    matrix = tiles[0, 0]
    tile_count, edge = matrix.shape[0], matrix.shape[1]
    width, row_count = start_block.shape
    group_count = lax.axis_size("grp")
    owner_count = lax.axis_size("row")
    owned = row_count // edge
    part = row_count // group_count
    columns = part // edge * owner_count
    total_cols = ITERS * width
    order = jnp.arange(tile_count, dtype=jnp.int32)
    position = tile_rows[0, 0] * columns + tile_cols[0, 0]
    here = (position[None, :] == jnp.arange(owned * columns, dtype=jnp.int32)[:, None]) & (
        order < live_tiles[0, 0]
    )[None, :]
    place = jnp.sum(jnp.where(here, order[None, :] + 1, 0), axis=1).astype(jnp.int32)

    vmem = pl.BlockSpec(memory_space=pltpu.VMEM)
    smem = pl.BlockSpec(memory_space=pltpu.SMEM)
    dma = pltpu.SemaphoreType.DMA
    packed = width + width * width // 128
    grp_sem = dma((group_count,))
    row_sem = dma((owner_count,))
    row_pair = dma((2, owner_count))
    shapes = (
            jax.ShapeDtypeStruct((ITERS, width, total_cols), jnp.float32),
            jax.ShapeDtypeStruct((ITERS, width, width), jnp.float32),
            jax.ShapeDtypeStruct((width, row_count), jnp.float32),
    )
    outs = pl.pallas_call(
        functools.partial(kernel, ITERS, group_count, owner_count),
        out_shape=shapes,
        in_specs=[vmem, vmem, smem, pl.BlockSpec(memory_space=pl.ANY)],
        out_specs=(vmem, vmem, vmem),
        scratch_shapes=[
            pltpu.VMEM(matrix.shape, jnp.bfloat16),
            pltpu.VMEM((owner_count, row_count, part), jnp.bfloat16),
            pltpu.VMEM((2, owner_count, 2 * width, part), jnp.bfloat16),
            pltpu.VMEM((group_count, 2 * width, part), jnp.bfloat16),
            pltpu.VMEM((owner_count // 2, width, part), jnp.float32),
            pltpu.VMEM((2, owner_count // 2, width, part), jnp.float32),
            pltpu.VMEM((group_count, width, part), jnp.float32),
            pltpu.VMEM((group_count, width, part), jnp.float32),
            pltpu.VMEM((owner_count // 2, width, part), jnp.float32),
            pltpu.VMEM((2, owner_count // 2, width, part), jnp.float32),
            pltpu.VMEM((2, 2, packed, total_cols), jnp.float32),
            pltpu.VMEM((group_count, packed, total_cols), jnp.float32),
            pltpu.VMEM((2, owner_count // 2, packed, total_cols), jnp.float32),
            pltpu.VMEM((total_cols, part), jnp.float32),
            pltpu.VMEM((total_cols, part), jnp.float32),
            pltpu.VMEM((width, part), jnp.float32),
            pltpu.VMEM((group_count, width, part), jnp.float32),
            pltpu.SemaphoreType.DMA,
            row_sem, row_pair, grp_sem, grp_sem,
            row_sem, row_pair, grp_sem, grp_sem,
            grp_sem, grp_sem, row_sem, row_pair, grp_sem, grp_sem,
            row_sem, row_sem, row_pair, dma, dma((2,)),
        ],
        compiler_params=pltpu.CompilerParams(
            collective_id=0, has_side_effects=True, vmem_limit_bytes=60 * 1024 * 1024
        ),
    )(start_block, dual_shift[None, :], place, matrix)
    return pl.pallas_call(hand_on, out_shape=shapes, in_specs=[vmem] * 3, out_specs=(vmem,) * 3)(*outs)


def solution(mesh):
    in_specs = (
        P("grp", "row", None, None, None),
        P("grp", "row", None),
        P("grp", "row", None),
        P("grp", "row"),
        P("row"),
        P(None, "row"),
    )
    out_specs = (P(), P(), P(None, "row"))
    return jax.shard_map(
        per_device, mesh=mesh, in_specs=in_specs, out_specs=out_specs, check_vma=False
    )
```

time: 113 us -> 88.6 us (0.78)
  Pallas kernels: 106 us -> 85.8 us
  local copies, waits for them, and re-layouts: 4.51 us -> 0 us
    pallas_call x1, Pallas kernels: 106 us -> 84.1 us  [per_device(): pl.pallas_call(functools.partial(kernel, ITERS, group_count, owner_count)...]
    unnamed x3 -> x0, local copies, waits for them, and re-layouts: 4.51 us -> none
    pallas_call x0 -> x1, Pallas kernels: none -> 1.68 us  [per_device(): pl.pallas_call(hand_on, out_shape=shapes, in_specs=[vmem] * 3, out_specs=...]
where the time goes in v2:
time: 88.6 us; the launch traced here: 88.4 us
  Pallas kernels  85.8 us (97%)
  other arithmetic  1.32 us (1%)
  between operations  1.29 us (1%)
    pallas_call x1, Pallas kernels, per_device(): pl.pallas_call(functools.partial(kernel, ITERS, group_count, owner_count)...  84.1 us

profile of v2, /device:TPU:0, one launch (start us, length us, event | category | flops | bytes accessed | tf_op | source)
XLA Modules:
  0.0 88.4 jit_solution(1161057641475002031)
XLA Ops:
  1.3 0.7 add_bitcast_fusion
  2.0 0.6 select_reduce_fusion.place_ref
  2.6 84.1 %shard_map.85 = (f32[4,32,128]{2,1,0:T(8,128)}, f32[4,32,32]{2,1,0:T(8,128)}, f32[32,1024]{1,0:T(8,128)}) custom-call(f32[32,1024]{1,0:T(8,128)} %start_ref.1, f32[1,1024]{1,0:T(1,128)} %bitcast.7, s32[32]{0:T(128)} %select_reduce_fusion.place_ref, bf16[32,256,256]{2,1,0:T(8,128)(2,1)} %bitcast.6), custom_call_target="tpu_custom_call" | custom-call | tf_op jit(solution)/shard_map/pallas_call | solution.py:354
  86.7 1.7 %shard_map.86 = (f32[4,32,128]{2,1,0:T(8,128)}, f32[4,32,32]{2,1,0:T(8,128)}, f32[32,1024]{1,0:T(8,128)}) custom-call(f32[4,32,128]{2,1,0:T(8,128)} %get-tuple-element.6.proj_in, f32[4,32,32]{2,1,0:T(8,128)} %get-tuple-element.7.fac_in, f32[32,1024]{1,0:T(8,128)} %get-tuple-element.8.next_in), custom_call_target="tpu_custom_call" | custom-call | tf_op jit(solution)/shard_map/pallas_call | solution.py:387
  (2 shorter events, 0.0 us)
